TPU v7x, 32 devices: a whole 2x2x4 slice. The times are simulated.
32 devices in a mesh: row: 4 (over x, core), col: 8 (over z, y).
Axes of the slice: x: 2, y: 2, z: 4, core: 2. Of those that a mesh axis runs over, the one named last changes fastest.
Arguments:
- tokens: bfloat16 [4, 1152, 8192], P('row', None, 'col'), may hold values from -64 to 64
- norm_gain: bfloat16 [8192], replicated, may hold values from 0.25 to 1.75
- w_query: bfloat16 [8192, 8192], P('row', 'col'), may hold values from -0.0625 to 0.0625
- w_keyval: bfloat16 [8192, 2048], P('row', 'col'), may hold values from -0.0625 to 0.0625
- kv_cache: bfloat16 [4, 8192, 2048], P('row', None, 'col'), may hold values from -96 to 96
- selected: int32 [4, 1152], P('row'), may hold values from 0 to 8192, as said below
- anchor: int32 [4, 16], P('row'), may hold values from 0 to 8191
Outputs:
- attended: bfloat16 [4, 1152, 8192], P('row', None, 'col')
Inputs may be any that keep to these rules, and one draw needn't show every extreme that they name: Each prompt's row lists distinct positions in increasing order, followed by entries equal to 8192 in the unused slots; at least three quarters of the 1152 slots of a prompt are used and some prompt uses all of them; selected positions fall unevenly over the spans.
All inputs are finite; a program needn't handle non-finite values.
Results may differ from a plain program's by a relative error of at most 0.006.
The roundings to bfloat16 on the way count: a program that leaves them out, or rounds other values in their place, can miss the bound.
Values may be sent and summed in bfloat16 or wider, within the bound.
A program may use at most 128 MiB of HBM per device.

v0:
```python
import functools
import math

import jax
import jax.numpy as jnp
from jax import lax
from jax.experimental import pallas as pl
from jax.experimental.pallas import tpu as pltpu
from jax.sharding import PartitionSpec as P

HD = 128
SPAN = 512
PAIR = 2
ONES = 16

rope_base = 500000.0
epsilon = 1e-05
masked_score = -1e30
MESH = pl.DeviceIdType.MESH
VMEM = pl.BlockSpec(memory_space=pltpu.VMEM)
ANY = pl.BlockSpec(memory_space=pl.ANY)


def angles(positions, width):
    half_width = width // 2
    exponents = jnp.arange(half_width, dtype=jnp.float32) * (-2.0 / width)
    frequency = jnp.exp(exponents * math.log(rope_base))
    phases = positions[..., None] * frequency
    phases = jnp.concatenate([phases, phases], axis=-1)
    return (jnp.cos(phases), jnp.sin(phases))


def turn(vectors, cosine, signed_sine):
    return vectors * cosine + pltpu.roll(vectors, HD // 2, 1) * signed_sine


def signed(sine_part):
    return sine_part * jnp.where(jnp.arange(HD) < HD // 2, -1.0, 1.0).astype(jnp.float32)


def project_kernel(
    cfg, tokens, gain, wq, wkv, cosine, sine, q_out, kv_out,
    x, weights_q, weights_kv, acc, rx, to_right, to_left, to_pair, local, w_send, w_recv,
):
    ncol, nrow, chunks = cfg
    length = ncol // PAIR
    slots, width = tokens.shape
    rows = slots // chunks
    detour = chunks // 2
    per_row = wq.shape[0]
    q_width = wq.shape[2]
    kv_width = wkv.shape[2]
    col = lax.axis_index("col")
    row = lax.axis_index("row")
    place = lax.div(col, PAIR)
    side = lax.rem(col, PAIR)
    other = 1 - side
    has_right = place + 1 < length
    has_left = place > 0
    right = {"col": lax.rem(col + PAIR, ncol)}
    left = {"col": lax.rem(col + ncol - PAIR, ncol)}
    pair = {"col": col + 1 - 2 * side}
    row_bits = list(reversed(range(nrow.bit_length() - 1)))

    def flipped(index, bit):
        step = 2**bit
        return index + step - 2 * step * lax.rem(lax.div(index, step), 2)

    barrier = pltpu.get_barrier_semaphore()
    neighbours = [right, left, pair] + [{"row": flipped(row, bit)} for bit in row_bits]
    for device in neighbours:
        pl.semaphore_signal(barrier, inc=1, device_id=device, device_id_type=MESH)
    pl.semaphore_wait(barrier, len(neighbours))

    def span(i):
        return pl.ds(pl.multiple_of(i * rows, rows), rows)

    def block(at, which):
        return at * PAIR + which

    def moved(device, sems, sem, at, which, i, own=False):
        here = x.at[block(at, which), span(i), :]
        return pltpu.make_async_remote_copy(
            src_ref=tokens.at[span(i), :] if own else here,
            dst_ref=here,
            send_sem=sems.at[sem, i],
            recv_sem=rx.at[block(at, which), i],
            device_id=device,
            device_id_type=MESH,
        )

    def arrived(at, which, i):
        moved(pair, to_pair, 0, at, which, i).wait_recv()

    @pl.loop(0, chunks)
    def _(i):
        @pl.when(has_right)
        def _():
            moved(right, to_right, place, place, side, i, True).start()

        @pl.when(has_left)
        def _():
            moved(left, to_left, place, place, side, i, True).start()

        moved(pair, to_pair, place, place, side, i, True).start()

    def weight_copy(bit, mask, number):
        owner = row
        for b in row_bits:
            if mask & 2**b:
                owner = flipped(owner, b)
        at = pl.ds(owner * per_row, per_row)
        pairs = [(wq, weights_q), (wkv, weights_kv)]
        return [
            pltpu.make_async_remote_copy(
                src_ref=source if mask == 0 else target.at[at],
                dst_ref=target.at[at],
                send_sem=w_send.at[number, j],
                recv_sem=w_recv.at[number, j],
                device_id={"row": flipped(row, bit)},
                device_id_type=MESH,
            )
            for j, (source, target) in enumerate(pairs)
        ]

    steps = []
    masks = [0]
    for bit in row_bits:
        steps += [(bit, mask) for mask in masks]
        masks += [mask ^ 2**bit for mask in masks]
    copies = [weight_copy(bit, mask, number) for number, (bit, mask) in enumerate(steps)]
    for (bit, mask), made in zip(steps, copies):
        if mask == 0:
            for copy in made:
                copy.start()
    mine = pl.ds(row * per_row, per_row)
    own_copies = [
        pltpu.make_async_copy(tokens, x.at[col], local.at[0]),
        pltpu.make_async_copy(wq, weights_q.at[mine], local.at[1]),
        pltpu.make_async_copy(wkv, weights_kv.at[mine], local.at[2]),
    ]
    for copy in own_copies:
        copy.start()

    def hand_on(distance, i):
        def forward(at, onward_ok, onward, sems):
            arrived(at, side, i)

            @pl.when(onward_ok)
            def _():
                moved(onward, sems, at, at, side, i).start()

            if distance == 1:
                @pl.when(i < detour)
                def _():
                    moved(pair, to_pair, at, at, side, i).start()
            else:
                moved(pair, to_pair, at, at, side, i).start()

        @pl.when(place >= distance)
        def _():
            forward(place - distance, has_right, right, to_right)

        @pl.when(place + distance < length)
        def _():
            forward(place + distance, has_left, left, to_left)

        if distance == 1:
            arrived(place, other, i)

    def project(i):
        for at in range(length):
            @pl.when(place != at)
            def _():
                arrived(at, other, i)

        def squares(b, total):
            part = x[b, span(i), :].astype(jnp.float32)
            part = part * part
            for k in range(0, width, HD):
                total = total + part[:, k : k + HD]
            return total

        total = lax.fori_loop(0, ncol, squares, jnp.zeros((rows, HD), jnp.float32))
        mean_square = jnp.sum(total, axis=1, keepdims=True) / (ncol * width)
        scale = lax.rsqrt(mean_square + epsilon)
        acc[...] = jnp.zeros(acc.shape, jnp.float32)

        @pl.loop(0, ncol)
        def _(b):
            part = x[b, span(i), :].astype(jnp.float32)
            normed = (part * scale * gain[pl.ds(b, 1), :]).astype(jnp.bfloat16)
            acc[:, :q_width] += jnp.dot(normed, weights_q[b], preferred_element_type=jnp.float32)
            acc[:, q_width:] += jnp.dot(normed, weights_kv[b], preferred_element_type=jnp.float32)

        cos, sin = cosine[span(i), :], sine[span(i), :]
        for h in range(0, q_width, HD):
            q_out[span(i), h : h + HD] = turn(acc[:, h : h + HD], cos, sin).astype(jnp.bfloat16)
        keys = acc[:, q_width : q_width + HD]
        turned = turn(keys, cos, sin)
        if kv_width == 2 * HD:
            kv_out[span(i), HD:] = acc[:, q_width + HD :].astype(jnp.bfloat16)
        else:
            turned = jnp.where(lax.rem(col, 2) == 0, turned, keys)
        kv_out[span(i), :HD] = turned.astype(jnp.bfloat16)

    for distance in range(1, length - 1):
        @pl.loop(0, chunks)
        def _(i):
            hand_on(distance, i)

    @pl.loop(detour, chunks)
    def _(i):
        @pl.when(has_right)
        def _():
            moved(right, to_right, length - 1, place, other, i).start()

        @pl.when(has_left)
        def _():
            moved(left, to_left, 0, place, other, i).start()

    for number, (bit, mask) in enumerate(steps):
        if mask:
            came = [m for m, (b, k) in enumerate(steps) if k ^ 2**b == mask][0]
            for copy in copies[came]:
                copy.wait_recv()
            for copy in copies[number]:
                copy.start()
    forwarded = {mask for _, mask in steps}
    for number, (bit, mask) in enumerate(steps):
        if mask ^ 2**bit not in forwarded:
            for copy in copies[number]:
                copy.wait_recv()
    for copy in own_copies:
        copy.wait()

    ahead = min(chunks, 4)

    @pl.loop(0, chunks + ahead)
    def _(i):
        @pl.when(i < chunks)
        def _():
            hand_on(length - 1, i)

        @pl.when(i >= ahead)
        def _():
            project(i - ahead)

    @pl.loop(0, chunks)
    def _(i):
        late = i >= detour
        for at in range(length):
            @pl.when(has_right & (place >= at))
            def _():
                moved(right, to_right, at, at, side, i).wait_send()

            @pl.when(has_left & (place <= at))
            def _():
                moved(left, to_left, at, at, side, i).wait_send()

            near = (place - at == 1) | (at - place == 1)

            @pl.when(jnp.logical_not(near & late))
            def _():
                moved(pair, to_pair, at, at, side, i).wait_send()

        @pl.when(late & has_right)
        def _():
            moved(right, to_right, length - 1, place, other, i).wait_send()

        @pl.when(late & has_left)
        def _():
            moved(left, to_left, 0, place, other, i).wait_send()

    for made in copies:
        for copy in made:
            copy.wait_send()


def gather_and_project(tokens, norm_gain, w_query, w_keyval, cosine, signed_sine):
    ncol, nrow = lax.axis_size("col"), lax.axis_size("row")
    slots, width = tokens.shape
    depth, q_width = w_query.shape
    kv_width = w_keyval.shape[1]
    chunks = next(n for n in (6, 4, 3, 2, 1) if slots % (n * 16) == 0)
    rows = slots // chunks
    features = ncol * width
    length = ncol // PAIR
    moves = nrow - 1
    dma = pltpu.SemaphoreType.DMA
    outs = (
        jax.ShapeDtypeStruct((slots, q_width), jnp.bfloat16),
        jax.ShapeDtypeStruct((slots, kv_width), jnp.bfloat16),
    )
    return pl.pallas_call(
        functools.partial(project_kernel, (ncol, nrow, chunks)),
        out_shape=outs,
        in_specs=[ANY, VMEM, ANY, ANY, VMEM, VMEM],
        out_specs=(VMEM, VMEM),
        scratch_shapes=[
            pltpu.VMEM((ncol, slots, width), jnp.bfloat16),
            pltpu.VMEM((ncol, width, q_width), jnp.bfloat16),
            pltpu.VMEM((ncol, width, kv_width), jnp.bfloat16),
            pltpu.VMEM((rows, q_width + kv_width), jnp.float32),
            dma((ncol, chunks)),
            dma((length, chunks)),
            dma((length, chunks)),
            dma((length, chunks)),
            dma((3,)),
            dma((moves, 2)),
            dma((moves, 2)),
        ],
        compiler_params=pltpu.CompilerParams(
            collective_id=0, has_side_effects=True, vmem_limit_bytes=62 * 2**20
        ),
        cost_estimate=pl.CostEstimate(
            flops=2 * slots * features * (q_width + kv_width),
            bytes_accessed=2 * (slots * features + features * (q_width + kv_width)),
            transcendentals=0,
        ),
    )(
        tokens,
        norm_gain.astype(jnp.float32).reshape(ncol, width),
        w_query.reshape(depth // width, width, q_width),
        w_keyval.reshape(depth // width, width, kv_width),
        cosine,
        signed_sine,
    )


def attend_kernel(cfg, bounds, edges, q, fresh, cache, chosen, chosen_row, acos, asin, out, keys, values, qt, m, acc):
    heads, length, wide, narrow, group = cfg
    block = pl.program_id(0)
    rows = q.shape[0]
    factor = HD ** (-0.5) * math.log2(math.e)
    spans = length // SPAN

    @pl.when(block == 0)
    def _():
        ones = jnp.ones((128, HD), jnp.bfloat16)

        def prepare(c, carry):
            base = pl.multiple_of(c * SPAN, SPAN)
            stored = cache[pl.ds(base, SPAN), :]
            old = stored[:, :HD].astype(jnp.float32)
            turned = old * acos[pl.ds(c, 1), :] + pltpu.roll(old, HD // 2, 1) * asin[pl.ds(c, 1), :]
            keys[pl.ds(base, SPAN), :HD] = turned.astype(jnp.bfloat16)
            keys[pl.ds(base, SPAN), HD:] = stored[:, HD:]

            def blend(tile, carry):
                at = pl.multiple_of(tile * 128, 128)
                place = base + lax.broadcasted_iota(jnp.int32, (SPAN, 128), 0)
                hits = (place == chosen_row[:, pl.ds(at, 128)]).astype(jnp.float32).astype(jnp.bfloat16)
                fresh_tile = jnp.concatenate([fresh[pl.ds(at, 128), :], ones], axis=1)
                placed = jnp.dot(hits, fresh_tile, preferred_element_type=jnp.float32)
                hit = placed[:, 2 * HD :] > 0.5
                for k in (0, HD):
                    before = keys[pl.ds(base, SPAN), k : k + HD].astype(jnp.float32)
                    after = jnp.where(hit, placed[:, k : k + HD], before)
                    keys[pl.ds(base, SPAN), k : k + HD] = after.astype(jnp.bfloat16)
                return carry

            lax.fori_loop(edges[c] // 128, (edges[c + 1] + 127) // 128, blend, 0)
            values[:HD, pl.ds(base, SPAN)] = keys[pl.ds(base, SPAN), HD:].astype(jnp.float32).T.astype(jnp.bfloat16)
            values[HD:, pl.ds(base, SPAN)] = jnp.ones((ONES, SPAN), jnp.bfloat16)
            keys[pl.ds(base, SPAN), HD:] = keys[pl.ds(base, SPAN), :HD]
            return carry

        lax.fori_loop(0, spans, prepare, 0)

    for h in range(heads):
        scaled = (q[:, h * HD : (h + 1) * HD].astype(jnp.float32) * factor).T
        high = scaled.astype(jnp.bfloat16)
        qt[:HD, h * rows : (h + 1) * rows] = high
        qt[HD:, h * rows : (h + 1) * rows] = (scaled - high.astype(jnp.float32)).astype(jnp.bfloat16)
    m[...] = jnp.full(m.shape, masked_score, jnp.float32)
    acc[...] = jnp.zeros(acc.shape, jnp.float32)
    limit = chosen[...]
    limits = jnp.concatenate([limit] * (group // rows), axis=1) if group > rows else limit

    def advance(size, masked, index, carry):
        start = pl.multiple_of(index * size, size)
        key_block = keys[pl.ds(start, size), :]
        value_block = values[:, pl.ds(start, size)]
        for at in range(0, heads * rows, group):
            scores = jnp.dot(key_block, qt[:, at : at + group], preferred_element_type=jnp.float32)
            if masked:
                place = start + lax.broadcasted_iota(jnp.int32, scores.shape, 0)
                scores = jnp.where(place <= limits, scores, masked_score)
            old = m[:, at : at + group]
            new = jnp.maximum(old, jnp.max(scores, axis=0, keepdims=True))
            weights = jnp.exp2(scores - new).astype(jnp.bfloat16)
            part = jnp.dot(value_block, weights, preferred_element_type=jnp.float32)
            acc[:, at : at + group] = acc[:, at : at + group] * jnp.exp2(old - new) + part
            m[:, at : at + group] = new
        return carry

    full, total = bounds[block, 0], bounds[block, 1]
    lax.fori_loop(0, full, functools.partial(advance, wide, False), 0)
    lax.fori_loop(full * (wide // narrow), total, functools.partial(advance, narrow, True), 0)
    for h in range(heads):
        part = acc[:, h * rows : (h + 1) * rows]
        outcome = jnp.where(limit < length, part[:HD, :] / part[HD : HD + 1, :], 0.0)
        out[:, h * HD : (h + 1) * HD] = outcome.T.astype(out.dtype)


def attend(q, fresh, cache, chosen, anchor, rows=128, wide=2048, narrow=512, group=1024):
    slot_count, width = q.shape
    length = cache.shape[0]
    heads = width // HD
    blocks = slot_count // rows
    spans = length // SPAN
    signs = jnp.where(jnp.arange(HD) < HD // 2, -1.0, 1.0).astype(jnp.float32)
    offsets = jnp.arange(spans, dtype=jnp.int32) * SPAN - anchor
    acos, asin = angles(offsets.astype(jnp.float32), HD)
    grouped = chosen.reshape(blocks, rows)
    farthest = jnp.max(jnp.where(grouped < length, grouped, 0), axis=1)
    total = farthest // narrow + 1
    full = jnp.minimum((grouped[:, 0] + 1) // wide, (farthest + 1) // wide)
    bounds = jnp.stack([full, total], axis=1).astype(jnp.int32)
    marks = jnp.arange(spans + 1, dtype=jnp.int32) * SPAN
    edges = jnp.sum(chosen[None, :] < marks[:, None], axis=1).astype(jnp.int32)
    mine = lambda i, *_: (i, 0)
    across = lambda i, *_: (0, i)
    whole = lambda i, *_: (0, 0)
    R = heads * rows
    group = min(group, R)
    wide = wide if length % wide == 0 else narrow
    elements = slot_count * heads * length
    return pl.pallas_call(
        functools.partial(attend_kernel, (heads, length, wide, narrow, group)),
        grid_spec=pltpu.PrefetchScalarGridSpec(
            num_scalar_prefetch=2,
            grid=(blocks,),
            in_specs=[
                pl.BlockSpec((rows, width), mine),
                pl.BlockSpec(fresh.shape, whole),
                pl.BlockSpec(cache.shape, whole),
                pl.BlockSpec((1, rows), across),
                pl.BlockSpec((1, slot_count), whole),
                pl.BlockSpec((spans, HD), whole),
                pl.BlockSpec((spans, HD), whole),
            ],
            out_specs=pl.BlockSpec((rows, width), mine),
            scratch_shapes=[
                pltpu.VMEM((length, 2 * HD), jnp.bfloat16),
                pltpu.VMEM((HD + ONES, length), jnp.bfloat16),
                pltpu.VMEM((2 * HD, R), jnp.bfloat16),
                pltpu.VMEM((1, R), jnp.float32),
                pltpu.VMEM((HD + ONES, R), jnp.float32),
            ],
        ),
        out_shape=jax.ShapeDtypeStruct((slot_count, width), jnp.bfloat16),
        cost_estimate=pl.CostEstimate(
            flops=2 * elements * HD, bytes_accessed=16 * slot_count * width, transcendentals=elements // 2
        ),
        compiler_params=pltpu.CompilerParams(vmem_limit_bytes=60 * 2**20),
    )(bounds, edges, q, fresh, cache, chosen[None, :], chosen[None, :], acos, asin * signs)


def from_partner(value):
    pairs = [(source, source ^ 1) for source in range(lax.axis_size("col"))]
    return lax.ppermute(value, "col", pairs)


def shards(tokens, norm_gain, w_query, w_keyval, kv_cache, selected, anchor):
    chosen = selected[0]
    cosine, sine_part = angles(chosen.astype(jnp.float32), HD)
    queries, fresh = gather_and_project(
        tokens[0], norm_gain, w_query, w_keyval, cosine, signed(sine_part)
    )
    stored = kv_cache[0]
    if w_keyval.shape[1] == HD:
        holds_key = lax.axis_index("col") % 2 == 0

        def both(mine):
            partner = from_partner(mine)
            return jnp.concatenate(
                [jnp.where(holds_key, mine, partner), jnp.where(holds_key, partner, mine)], axis=1
            )

        stored, fresh = both(stored), both(fresh)
    return attend(queries, fresh, stored, chosen, anchor[0])[None]


def solution(mesh):
    in_specs = (
        P("row", None, "col"),
        P(),
        P("row", "col"),
        P("row", "col"),
        P("row", None, "col"),
        P("row", None),
        P("row", None),
    )
    out_specs = P("row", None, "col")
    return jax.shard_map(shards, mesh=mesh, in_specs=in_specs, out_specs=out_specs, check_vma=False)
```

profile of v0, /device:TPU:0, one launch (start us, length us, event | category | flops | bytes accessed | tf_op | source)
XLA Modules:
  0.0 306.7 jit_solution(9537355554063287740)
XLA Ops:
  0.0 0.7 fusion.11
  0.7 0.1 broadcast_multiply_fusion.1
  0.8 0.7 reduce
  1.5 0.8 convert_reduce_fusion.edges
  2.2 0.1 fusion.6
  2.3 0.1 copy.22
  2.5 0.7 pad_add_fusion.bounds
  3.1 0.7 sine_multiply_fusion.1
  3.9 1.3 reshape.149.gain
  5.2 0.2 broadcast_multiply_fusion
  5.4 3.3 %sine_multiply_fusion = (f32[1152,128]{1,0:T(8,128)}, f32[1152,128]{1,0:T(8,128)}) fusion(f32[1152,64]{1,0:T(8,128)S(1)} %broadcast_multiply_fusion, f32[128]{0:T(128)S(1)} %compare_select_fusion.1), kind=kLoop, calls=%fused_computation.1 | loop fusion | flops 294912 | bytes 1475072 | tf_op jit(solution)/shard_map/mul | solution.py:38
  8.7 197.5 %shard_map.73 = (bf16[1152,1024]{1,0:T(8,128)(2,1)}, bf16[1152,256]{1,0:T(8,128)(2,1)}) custom-call(bf16[1152,1024]{1,0:T(8,128)(2,1)} %bitcast.16, f32[8,1024]{1,0:T(8,128)} %reshape.149.gain, bf16[2,1024,1024]{2,1,0:T(8,128)(2,1)} %bitcast.14, bf16[2,1024,256]{2,1,0:T(8,128)(2,1)} %bitcast.17, f32[1152,128]{1,0:T(8,128)} %get-tuple-element.10.cosine, ...), custom_call_target="tpu_custom_call" | custom-call | flops 24159191040 | bytes 39845888 | tf_op jit(solution)/shard_map/pallas_call | solution.py:295
  206.2 100.5 %shard_map.74 = bf16[1152,1024]{1,0:T(8,128)(2,1)} custom-call(s32[9,2]{1,0:T(8,128)} %pad_add_fusion.bounds, s32[17]{0:T(128)} %convert_reduce_fusion.edges, bf16[1152,1024]{1,0:T(8,128)(2,1)} %get-tuple-element.7.q, bf16[1152,256]{1,0:T(8,128)(2,1)} %get-tuple-element.8.fresh, bf16[8192,256]{1,0:T(8,128)(2,1)} %bitcast.15, s32[1,1152]{1,0:T(1,128)} %chosen_row.1, ...), custom_call_target="tpu_custom_call" | custom-call | flops 19327352832 | bytes 18874368 | tf_op jit(solution)/shard_map/pallas_call | solution.py:430
  (5 shorter events, 0.0 us)
where the time goes:
time: 307 us
  Pallas kernels  298 us (97%)
  other arithmetic  7.24 us (2%)
    pallas_call x1, Pallas kernels, gather_and_project(): pl.pallas_call(functools.partial(project_kernel, (ncol, nrow, chunks)), o...  198 us
    pallas_call x1, Pallas kernels, attend(): pl.pallas_call(functools.partial(attend_kernel, (heads, length, wide, nar...  100 us

commit v1 on v0

--- a/solution.py
+++ b/solution.py
@@ -12,6 +12,7 @@
 SPAN = 512
 PAIR = 2
 ONES = 16
+TILE = 128
 
 rope_base = 500000.0
 epsilon = 1e-05
@@ -21,35 +22,22 @@
 ANY = pl.BlockSpec(memory_space=pl.ANY)
 
 
-def angles(positions, width):
-    half_width = width // 2
-    exponents = jnp.arange(half_width, dtype=jnp.float32) * (-2.0 / width)
-    frequency = jnp.exp(exponents * math.log(rope_base))
-    phases = positions[..., None] * frequency
-    phases = jnp.concatenate([phases, phases], axis=-1)
-    return (jnp.cos(phases), jnp.sin(phases))
-
-
 def turn(vectors, cosine, signed_sine):
     return vectors * cosine + pltpu.roll(vectors, HD // 2, 1) * signed_sine
 
 
-def signed(sine_part):
-    return sine_part * jnp.where(jnp.arange(HD) < HD // 2, -1.0, 1.0).astype(jnp.float32)
-
-
 def project_kernel(
-    cfg, tokens, gain, wq, wkv, cosine, sine, q_out, kv_out,
-    x, weights_q, weights_kv, acc, rx, to_right, to_left, to_pair, local, w_send, w_recv,
+    cfg, tokens, gain, wq, wkv, chosen, q_out, kv_out, edges, firsts, lasts,
+    x, weights_q, weights_kv, normed, cosine, sine, rx, to_right, to_left, to_pair, local, w_send, w_recv,
 ):
-    ncol, nrow, chunks = cfg
+    ncol, nrow, chunks, total_length = cfg
     length = ncol // PAIR
     slots, width = tokens.shape
     rows = slots // chunks
     detour = chunks // 2
     per_row = wq.shape[0]
-    q_width = wq.shape[2]
-    kv_width = wkv.shape[2]
+    q_width = wq.shape[1]
+    kv_width = wkv.shape[1]
     col = lax.axis_index("col")
     row = lax.axis_index("row")
     place = lax.div(col, PAIR)
@@ -109,7 +97,7 @@
         for b in row_bits:
             if mask & 2**b:
                 owner = flipped(owner, b)
-        at = pl.ds(owner * per_row, per_row)
+        at = pl.ds(pl.multiple_of(owner * per_row, per_row), per_row)
         pairs = [(wq, weights_q), (wkv, weights_kv)]
         return [
             pltpu.make_async_remote_copy(
@@ -133,7 +121,7 @@
         if mask == 0:
             for copy in made:
                 copy.start()
-    mine = pl.ds(row * per_row, per_row)
+    mine = pl.ds(pl.multiple_of(row * per_row, per_row), per_row)
     own_copies = [
         pltpu.make_async_copy(tokens, x.at[col], local.at[0]),
         pltpu.make_async_copy(wq, weights_q.at[mine], local.at[1]),
@@ -142,6 +130,26 @@
     for copy in own_copies:
         copy.start()
 
+    index = lax.broadcasted_iota(jnp.int32, (HD, TILE), 0)
+    half = lax.rem(index, HD // 2).astype(jnp.float32)
+    frequency = jnp.exp(half * (-2.0 / HD) * math.log(rope_base))
+    sign = jnp.where(lax.broadcasted_iota(jnp.int32, (TILE, HD), 1) < HD // 2, -1.0, 1.0)
+    marks = (lax.broadcasted_iota(jnp.int32, edges.shape, 0) * SPAN).astype(jnp.float32)
+    below = jnp.zeros(edges.shape, jnp.float32)
+    for t in range(slots // TILE):
+        at = slice(t * TILE, (t + 1) * TILE)
+        positions = chosen[:, at].astype(jnp.float32)
+        phases = positions * frequency
+        cosine[at, :] = jnp.cos(phases).T
+        sine[at, :] = jnp.sin(phases).T * sign
+        below = below + jnp.where(positions < marks, 1.0, 0.0)
+        first = jnp.min(positions, axis=1, keepdims=True)
+        last = jnp.max(jnp.where(positions < total_length, positions, 0.0), axis=1, keepdims=True)
+        firsts[t : t + 1, :] = jnp.broadcast_to(first, (1, TILE)).astype(jnp.int32)
+        lasts[t : t + 1, :] = jnp.broadcast_to(last, (1, TILE)).astype(jnp.int32)
+    below = jnp.sum(below, axis=1, keepdims=True)
+    edges[...] = jnp.broadcast_to(below, edges.shape).astype(jnp.int32)
+
     def hand_on(distance, i):
         def forward(at, onward_ok, onward, sems):
             arrived(at, side, i)
@@ -169,11 +177,6 @@
             arrived(place, other, i)
 
     def project(i):
-        for at in range(length):
-            @pl.when(place != at)
-            def _():
-                arrived(at, other, i)
-
         def squares(b, total):
             part = x[b, span(i), :].astype(jnp.float32)
             part = part * part
@@ -181,25 +184,41 @@
                 total = total + part[:, k : k + HD]
             return total
 
-        total = lax.fori_loop(0, ncol, squares, jnp.zeros((rows, HD), jnp.float32))
+        total = jnp.zeros((rows, HD), jnp.float32)
+        for at in range(length):
+            total = squares(block(at, side), total)
+        for at in range(length):
+            @pl.when(place != at)
+            def _():
+                arrived(at, other, i)
+        for at in range(length):
+            total = squares(block(at, other), total)
         mean_square = jnp.sum(total, axis=1, keepdims=True) / (ncol * width)
         scale = lax.rsqrt(mean_square + epsilon)
-        acc[...] = jnp.zeros(acc.shape, jnp.float32)
-
-        @pl.loop(0, ncol)
-        def _(b):
+        cos, sin = cosine[span(i), :], sine[span(i), :]
+
+        def heads(result, first):
+            for k in range(0, result.shape[1], HD):
+                part = turn(result[:, k : k + HD], cos, sin)
+                q_out[span(i), first + k : first + k + HD] = part.astype(jnp.bfloat16)
+
+        step = min(2 * HD, q_width)
+        result = jnp.zeros((rows, step), jnp.float32)
+        for b in range(ncol):
+            at = slice(b * width, (b + 1) * width)
             part = x[b, span(i), :].astype(jnp.float32)
-            normed = (part * scale * gain[pl.ds(b, 1), :]).astype(jnp.bfloat16)
-            acc[:, :q_width] += jnp.dot(normed, weights_q[b], preferred_element_type=jnp.float32)
-            acc[:, q_width:] += jnp.dot(normed, weights_kv[b], preferred_element_type=jnp.float32)
-
-        cos, sin = cosine[span(i), :], sine[span(i), :]
-        for h in range(0, q_width, HD):
-            q_out[span(i), h : h + HD] = turn(acc[:, h : h + HD], cos, sin).astype(jnp.bfloat16)
-        keys = acc[:, q_width : q_width + HD]
+            part = (part * scale * gain[:, at].astype(jnp.float32)).astype(jnp.bfloat16)
+            normed[:, at] = part
+            result = result + jnp.dot(part, weights_q[at, :step], preferred_element_type=jnp.float32)
+        heads(result, 0)
+        for first in range(step, q_width, step):
+            columns = weights_q[:, first : first + step]
+            heads(jnp.dot(normed[...], columns, preferred_element_type=jnp.float32), first)
+        result = jnp.dot(normed[...], weights_kv[...], preferred_element_type=jnp.float32)
+        keys = result[:, :HD]
         turned = turn(keys, cos, sin)
         if kv_width == 2 * HD:
-            kv_out[span(i), HD:] = acc[:, q_width + HD :].astype(jnp.bfloat16)
+            kv_out[span(i), HD:] = result[:, HD:].astype(jnp.bfloat16)
         else:
             turned = jnp.where(lax.rem(col, 2) == 0, turned, keys)
         kv_out[span(i), :HD] = turned.astype(jnp.bfloat16)
@@ -277,7 +296,7 @@
             copy.wait_send()
 
 
-def gather_and_project(tokens, norm_gain, w_query, w_keyval, cosine, signed_sine):
+def gather_and_project(tokens, norm_gain, w_query, w_keyval, selected, total_length):
     ncol, nrow = lax.axis_size("col"), lax.axis_size("row")
     slots, width = tokens.shape
     depth, q_width = w_query.shape
@@ -291,17 +310,22 @@
     outs = (
         jax.ShapeDtypeStruct((slots, q_width), jnp.bfloat16),
         jax.ShapeDtypeStruct((slots, kv_width), jnp.bfloat16),
+        jax.ShapeDtypeStruct((-(-(total_length // SPAN + 1) // 8) * 8, TILE), jnp.int32),
+        jax.ShapeDtypeStruct((slots // TILE, TILE), jnp.int32),
+        jax.ShapeDtypeStruct((slots // TILE, TILE), jnp.int32),
     )
     return pl.pallas_call(
-        functools.partial(project_kernel, (ncol, nrow, chunks)),
+        functools.partial(project_kernel, (ncol, nrow, chunks, total_length)),
         out_shape=outs,
-        in_specs=[ANY, VMEM, ANY, ANY, VMEM, VMEM],
-        out_specs=(VMEM, VMEM),
+        in_specs=[ANY, VMEM, ANY, ANY, VMEM],
+        out_specs=(VMEM,) * 5,
         scratch_shapes=[
             pltpu.VMEM((ncol, slots, width), jnp.bfloat16),
-            pltpu.VMEM((ncol, width, q_width), jnp.bfloat16),
-            pltpu.VMEM((ncol, width, kv_width), jnp.bfloat16),
-            pltpu.VMEM((rows, q_width + kv_width), jnp.float32),
+            pltpu.VMEM((features, q_width), jnp.bfloat16),
+            pltpu.VMEM((features, kv_width), jnp.bfloat16),
+            pltpu.VMEM((rows, features), jnp.bfloat16),
+            pltpu.VMEM((slots, HD), jnp.float32),
+            pltpu.VMEM((slots, HD), jnp.float32),
             dma((ncol, chunks)),
             dma((length, chunks)),
             dma((length, chunks)),
@@ -320,15 +344,16 @@
         ),
     )(
         tokens,
-        norm_gain.astype(jnp.float32).reshape(ncol, width),
-        w_query.reshape(depth // width, width, q_width),
-        w_keyval.reshape(depth // width, width, kv_width),
-        cosine,
-        signed_sine,
+        norm_gain[None, :],
+        w_query,
+        w_keyval,
+        selected,
     )
 
 
-def attend_kernel(cfg, bounds, edges, q, fresh, cache, chosen, chosen_row, acos, asin, out, keys, values, qt, m, acc):
+def attend_kernel(
+    cfg, edges, firsts, lasts, anchor, q, fresh, cache, chosen, chosen_row, out, keys, values, qt, m, acc, acos, asin
+):
     heads, length, wide, narrow, group = cfg
     block = pl.program_id(0)
     rows = q.shape[0]
@@ -337,7 +362,14 @@
 
     @pl.when(block == 0)
     def _():
-        ones = jnp.ones((128, HD), jnp.bfloat16)
+        ones = jnp.ones((TILE, HD), jnp.bfloat16)
+        for c in range(spans):
+            acos[c : c + 1, :] = jnp.full((1, HD), (c * SPAN - anchor[0, c]).astype(jnp.float32))
+        lane = lax.broadcasted_iota(jnp.int32, acos.shape, 1)
+        half = lax.rem(lane, HD // 2).astype(jnp.float32)
+        phases = acos[...] * jnp.exp(half * (-2.0 / HD) * math.log(rope_base))
+        asin[...] = jnp.sin(phases) * jnp.where(lane < HD // 2, -1.0, 1.0)
+        acos[...] = jnp.cos(phases)
 
         def prepare(c, carry):
             base = pl.multiple_of(c * SPAN, SPAN)
@@ -348,10 +380,10 @@
             keys[pl.ds(base, SPAN), HD:] = stored[:, HD:]
 
             def blend(tile, carry):
-                at = pl.multiple_of(tile * 128, 128)
-                place = base + lax.broadcasted_iota(jnp.int32, (SPAN, 128), 0)
-                hits = (place == chosen_row[:, pl.ds(at, 128)]).astype(jnp.float32).astype(jnp.bfloat16)
-                fresh_tile = jnp.concatenate([fresh[pl.ds(at, 128), :], ones], axis=1)
+                at = pl.multiple_of(tile * TILE, TILE)
+                place = base + lax.broadcasted_iota(jnp.int32, (SPAN, TILE), 0)
+                hits = (place == chosen_row[:, pl.ds(at, TILE)]).astype(jnp.float32).astype(jnp.bfloat16)
+                fresh_tile = jnp.concatenate([fresh[pl.ds(at, TILE), :], ones], axis=1)
                 placed = jnp.dot(hits, fresh_tile, preferred_element_type=jnp.float32)
                 hit = placed[:, 2 * HD :] > 0.5
                 for k in (0, HD):
@@ -360,7 +392,7 @@
                     keys[pl.ds(base, SPAN), k : k + HD] = after.astype(jnp.bfloat16)
                 return carry
 
-            lax.fori_loop(edges[c] // 128, (edges[c + 1] + 127) // 128, blend, 0)
+            lax.fori_loop(edges[c, 0] // TILE, (edges[c + 1, 0] + TILE - 1) // TILE, blend, 0)
             values[:HD, pl.ds(base, SPAN)] = keys[pl.ds(base, SPAN), HD:].astype(jnp.float32).T.astype(jnp.bfloat16)
             values[HD:, pl.ds(base, SPAN)] = jnp.ones((ONES, SPAN), jnp.bfloat16)
             keys[pl.ds(base, SPAN), HD:] = keys[pl.ds(base, SPAN), :HD]
@@ -395,7 +427,9 @@
             m[:, at : at + group] = new
         return carry
 
-    full, total = bounds[block, 0], bounds[block, 1]
+    farthest = lasts[block, 0]
+    total = farthest // narrow + 1
+    full = jnp.minimum((firsts[block, 0] + 1) // wide, (farthest + 1) // wide)
     lax.fori_loop(0, full, functools.partial(advance, wide, False), 0)
     lax.fori_loop(full * (wide // narrow), total, functools.partial(advance, narrow, True), 0)
     for h in range(heads):
@@ -404,33 +438,25 @@
         out[:, h * HD : (h + 1) * HD] = outcome.T.astype(out.dtype)
 
 
-def attend(q, fresh, cache, chosen, anchor, rows=128, wide=2048, narrow=512, group=1024):
+def attend(q, fresh, cache, selected, anchor, edges, firsts, lasts):
     slot_count, width = q.shape
     length = cache.shape[0]
     heads = width // HD
+    rows = TILE
     blocks = slot_count // rows
     spans = length // SPAN
-    signs = jnp.where(jnp.arange(HD) < HD // 2, -1.0, 1.0).astype(jnp.float32)
-    offsets = jnp.arange(spans, dtype=jnp.int32) * SPAN - anchor
-    acos, asin = angles(offsets.astype(jnp.float32), HD)
-    grouped = chosen.reshape(blocks, rows)
-    farthest = jnp.max(jnp.where(grouped < length, grouped, 0), axis=1)
-    total = farthest // narrow + 1
-    full = jnp.minimum((grouped[:, 0] + 1) // wide, (farthest + 1) // wide)
-    bounds = jnp.stack([full, total], axis=1).astype(jnp.int32)
-    marks = jnp.arange(spans + 1, dtype=jnp.int32) * SPAN
-    edges = jnp.sum(chosen[None, :] < marks[:, None], axis=1).astype(jnp.int32)
+    narrow = SPAN
+    wide = next(n for n in (4 * SPAN, 2 * SPAN, SPAN) if length % n == 0)
+    group = heads * rows
     mine = lambda i, *_: (i, 0)
     across = lambda i, *_: (0, i)
     whole = lambda i, *_: (0, 0)
     R = heads * rows
-    group = min(group, R)
-    wide = wide if length % wide == 0 else narrow
     elements = slot_count * heads * length
     return pl.pallas_call(
         functools.partial(attend_kernel, (heads, length, wide, narrow, group)),
         grid_spec=pltpu.PrefetchScalarGridSpec(
-            num_scalar_prefetch=2,
+            num_scalar_prefetch=4,
             grid=(blocks,),
             in_specs=[
                 pl.BlockSpec((rows, width), mine),
@@ -438,8 +464,6 @@
                 pl.BlockSpec(cache.shape, whole),
                 pl.BlockSpec((1, rows), across),
                 pl.BlockSpec((1, slot_count), whole),
-                pl.BlockSpec((spans, HD), whole),
-                pl.BlockSpec((spans, HD), whole),
             ],
             out_specs=pl.BlockSpec((rows, width), mine),
             scratch_shapes=[
@@ -448,6 +472,8 @@
                 pltpu.VMEM((2 * HD, R), jnp.bfloat16),
                 pltpu.VMEM((1, R), jnp.float32),
                 pltpu.VMEM((HD + ONES, R), jnp.float32),
+                pltpu.VMEM((spans, HD), jnp.float32),
+                pltpu.VMEM((spans, HD), jnp.float32),
             ],
         ),
         out_shape=jax.ShapeDtypeStruct((slot_count, width), jnp.bfloat16),
@@ -455,7 +481,7 @@
             flops=2 * elements * HD, bytes_accessed=16 * slot_count * width, transcendentals=elements // 2
         ),
         compiler_params=pltpu.CompilerParams(vmem_limit_bytes=60 * 2**20),
-    )(bounds, edges, q, fresh, cache, chosen[None, :], chosen[None, :], acos, asin * signs)
+    )(edges, firsts, lasts, anchor, q, fresh, cache, selected, selected)
 
 
 def from_partner(value):
@@ -464,12 +490,10 @@
 
 
 def shards(tokens, norm_gain, w_query, w_keyval, kv_cache, selected, anchor):
-    chosen = selected[0]
-    cosine, sine_part = angles(chosen.astype(jnp.float32), HD)
-    queries, fresh = gather_and_project(
-        tokens[0], norm_gain, w_query, w_keyval, cosine, signed(sine_part)
+    stored = kv_cache[0]
+    queries, fresh, *tables = gather_and_project(
+        tokens[0], norm_gain, w_query, w_keyval, selected, stored.shape[0]
     )
-    stored = kv_cache[0]
     if w_keyval.shape[1] == HD:
         holds_key = lax.axis_index("col") % 2 == 0
 
@@ -480,7 +504,7 @@
             )
 
         stored, fresh = both(stored), both(fresh)
-    return attend(queries, fresh, stored, chosen, anchor[0])[None]
+    return attend(queries, fresh, stored, selected, anchor, *tables)[None]
 
 
 def solution(mesh):

time: 307 us -> 285 us (0.928)
  the two profiles are of different devices: /device:TPU:0 before, /device:TPU:2 now
where the time goes in v1:
time: 285 us; the launch traced here: 282 us
  Pallas kernels  281 us (99%)
    pallas_call x1, Pallas kernels, gather_and_project(): pl.pallas_call(functools.partial(project_kernel, (ncol, nrow, chunks, tot...  191 us
    pallas_call x1, Pallas kernels, attend(): pl.pallas_call(functools.partial(attend_kernel, (heads, length, wide, nar...  89.4 us

profile of v1, /device:TPU:2, one launch (start us, length us, event | category | flops | bytes accessed | tf_op | source)
XLA Modules:
  0.0 282.0 jit_solution(10333043901904546261)
XLA Ops:
  0.0 1.3 broadcast_in_dim.6.gain
  1.4 191.3 %shard_map.73 = (bf16[1152,1024]{1,0:T(8,128)(2,1)}, bf16[1152,256]{1,0:T(8,128)(2,1)}, s32[24,128]{1,0:T(8,128)}, s32[9,128]{1,0:T(8,128)}, s32[9,128]{1,0:T(8,128)}) custom-call(bf16[1152,1024]{1,0:T(8,128)(2,1)} %bitcast.4, bf16[1,8192]{1,0:T(2,128)(2,1)} %broadcast_in_dim.6.gain, bf16[2048,1024]{1,0:T(8,128)(2,1)} %wq.1, bf16[2048,256]{1,0:T(8,128)(2,1)} %wkv.1, ...), custom_call_target="tpu_custom_call" | custom-call | flops 24159191040 | bytes 39845888 | tf_op jit(solution)/shard_map/pallas_call | solution.py:317
  192.6 89.4 %shard_map.74 = bf16[1152,1024]{1,0:T(8,128)(2,1)} custom-call(s32[24,128]{1,0:T(8,128)} %get-tuple-element.10.edges, s32[9,128]{1,0:T(8,128)} %get-tuple-element.11.firsts, s32[9,128]{1,0:T(8,128)} %get-tuple-element.12.lasts, s32[1,16]{1,0:T(1,128)} %anchor.1, bf16[1152,1024]{1,0:T(8,128)(2,1)} %get-tuple-element.13.q, ...), custom_call_target="tpu_custom_call" | custom-call | flops 19327352832 | bytes 18874368 | tf_op jit(solution)/shard_map/pallas_call | solution.py:456
